TPU v7x, 32 devices: a whole 2x2x4 slice. The times are simulated.
32 devices in a mesh: freq: 2 (over core), row: 4 (over y, x), col: 4 (over z).
Axes of the slice: x: 2, y: 2, z: 4, core: 2. Of those that a mesh axis runs over, the one named last changes fastest.
Arguments:
- coupling: bfloat16 [6144, 6144], P('row', 'col'), may hold values from -0.15625 to 0.15625
- freq_weight: float32 [12288], P(('freq', 'row')), parts along dimension 0, may hold values from 0.05 to 2
Outputs:
- response: float32 [12288, 6144], P(('freq', 'row'), 'col'), parts along dimension 0
There are 2 independent parts, one for each index of `freq`. A program takes and returns all parts, laid end to end along the dimension named above; an argument that names none is the same for every part. Nothing has to cross between parts.
All inputs are finite; a program needn't handle non-finite values.
Results may differ from a plain program's by a relative error of at most 0.0021.
Values may be sent and summed in bfloat16 or wider, within the bound.
A program may use at most 128 MiB of HBM per device.

v0:
```python
import jax
import jax.numpy as jnp
from jax import lax
from jax.sharding import PartitionSpec as P


def on_device(coupling, freq_weight):
    weighted = (coupling.astype(jnp.float32) * freq_weight[:, None]).astype(jnp.bfloat16)
    full_rows = lax.all_gather(weighted, "col", axis=1, tiled=True)
    return lax.psum_scatter(
        lax.dot_general(
            full_rows, coupling, (((0,), (0,)), ((), ())), preferred_element_type=jnp.float32
        ),
        "row",
        scatter_dimension=0,
        tiled=True,
    )


def solution(mesh):
    placed = (P("row", "col"), P(("freq", "row")))
    return jax.shard_map(
        on_device, mesh=mesh, in_specs=placed, out_specs=P(("freq", "row"), "col"), check_vma=False
    )
```

profile of v0, /device:TPU:6, one launch (start us, length us, event | category | flops | bytes accessed | tf_op | source)
XLA Modules:
  0.0 699.9 jit_solution(10874687154043378415)
XLA Ops:
  6.5 0.0 all-gather.2.cloned.1.call-start
  6.5 5.4 multiply_convert_fusion
  11.9 0.0 all-gather.2.cloned.1.call-update
  11.9 0.0 reduce-scatter.2.cloned.1.call-start
  12.0 323.8 %all-gather.2.cloned.1.call-done = bf16[1536,6144]{1,0:T(8,128)(2,1)} async-done(((bf16[1536,1536]{1,0:T(8,128)(2,1)}), bf16[1536,6144]{1,0:T(8,128)(2,1)}) %all-gather.2.cloned.1.call-update) | async-done | bytes 18874384 | tf_op jit(solution)/shard_map/all_gather | solution.py:9
  335.8 36.7 %fusion = f32[6144,1536]{1,0:T(8,128)} fusion(bf16[1536,6144]{1,0:T(8,128)(2,1)} %all-gather.2.cloned.1.call-done, bf16[1536,1536]{1,0:T(8,128)(2,1)} %param.2), kind=kOutput, calls=%fused_computation.1 | convolution fusion | flops 28991029248 | bytes 61341696 | tf_op jit(solution)/shard_map/dot_general | solution.py:11
  372.5 0.0 reduce-scatter.2.cloned.1.call-update
  372.6 320.5 %reduce-scatter.2.cloned.1.call-done = f32[1536,1536]{1,0:T(8,128)} async-done(((f32[6144,1536]{1,0:T(8,128)}), f32[1536,1536]{1,0:T(8,128)}) %reduce-scatter.2.cloned.1.call-update) | async-done | bytes 9437200 | tf_op jit(solution)/shard_map/reduce_scatter | solution.py:10
Async XLA Ops:
  6.5 329.3 %all-gather.2.cloned.1.call-start = ((), (), s32[]{:S(2)}) async-start(), calls=%async_computation.1 | async-start | bytes 23592960 | tf_op jit(solution)/shard_map/all_gather | solution.py:9
  11.9 681.2 %reduce-scatter.2.cloned.1.call-start = ((), (), s32[]{:S(2)}) async-start(), calls=%async_computation.2 | async-start | bytes 47185920 | tf_op jit(solution)/shard_map/reduce_scatter | solution.py:10
Sparse Core Ops, SparseCore 0:
  12.0 323.7 all-gather.1
  372.7 320.3 reduce-scatter.1
where the time goes:
time: 703 us; the launch traced here: 700 us
  waiting for transfers between devices  644 us (92%)
  matrix products  36.7 us (5%)
  between operations  13.4 us (2%)
    all_gather x1, waiting for transfers between devices, on_device(): full_rows = lax.all_gather(weighted, 'col', axis=1, tiled=True)  324 us
    reduce_scatter x1, waiting for transfers between devices, on_device(): lax.psum_scatter(lax.dot_general(full_rows, coupling, (((0,), (0,)), ((),...  321 us
    dot_general x1, matrix products, on_device(): lax.dot_general(full_rows, coupling, (((0,), (0,)), ((), ())), preferred_...  36.7 us
  transfers between devices with their start and end apart: 2, of which 2 were waited for; matrix products, arithmetic and copies ran while one was open for 0% of the time, Pallas kernels for 0%

commit v1 on v0

v1 whole, which is shorter than its diff:
```python
import functools

import jax
import jax.numpy as jnp
from jax import lax
from jax.experimental import pallas as pl
from jax.experimental.pallas import tpu as pltpu
from jax.sharding import PartitionSpec as P

MESH = pl.DeviceIdType.MESH
SIDE = 2


def kernel(cols_n, K, CH, c_ref, w_ref, o_ref, X, T, W, acc, load, wsend, wrecv, zr, zup, zdn, tl, nr, nx, ny, nrl,
           ms, mr, ds, dr, osem):
    f = lax.axis_index("freq")
    r = lax.axis_index("row")
    z = lax.axis_index("col")
    rows_n = SIDE * SIDE
    H = CH // 2
    other = 1 - f
    xn, yn, dg = r ^ 1, r ^ 2, r ^ 3
    plane = (xn, yn, dg)
    mi = jnp.where(r == z, 0, 1)
    width = c_ref.shape[1]

    def rows_of(k, core):
        return pl.ds(pl.multiple_of(k * CH + core * H, H), H)

    def trow(k):
        return pl.ds(pl.multiple_of(k * H, H), H)

    def rcopy(src, dst, s, d, dev):
        return pltpu.make_async_remote_copy(src_ref=src, dst_ref=dst, send_sem=s, recv_sem=d, device_id=dev,
                                            device_id_type=MESH)

    barrier = pltpu.get_barrier_semaphore()
    pl.semaphore_signal(barrier, inc=1, device_id={"freq": other}, device_id_type=MESH)
    for p in plane:
        pl.semaphore_signal(barrier, inc=1, device_id={"row": p}, device_id_type=MESH)

    @pl.when(z > 0)
    def _():
        pl.semaphore_signal(barrier, inc=1, device_id={"col": z - 1}, device_id_type=MESH)

    @pl.when(z < cols_n - 1)
    def _():
        pl.semaphore_signal(barrier, inc=1, device_id={"col": z + 1}, device_id_type=MESH)

    mine = X.at[0, r]
    own = pltpu.make_async_copy(c_ref, mine, load.at[0])
    own.start()
    wown = pltpu.make_async_copy(w_ref, W.at[r], load.at[1])
    wown.start()
    acc[...] = jnp.zeros_like(acc)
    own.wait()
    wown.wait()
    pl.semaphore_wait(barrier, 1 + len(plane) + jnp.where(z > 0, 1, 0) + jnp.where(z < cols_n - 1, 1, 0))

    def w_copy(i):
        return rcopy(W.at[r], W.at[r], wsend.at[i], wrecv.at[i], {"row": plane[i]})

    def zsrc(q, k):
        return T.at[q, trow(k)]

    def z_own(k, up):
        src = X.at[0, r, rows_of(k, f)]
        return rcopy(src, T.at[z, trow(k)], (zup if up else zdn).at[z, k], zr.at[z, k],
                     {"col": z + 1 if up else z - 1})

    def z_fwd(q, k, up):
        return rcopy(zsrc(q, k), zsrc(q, k), (zup if up else zdn).at[q, k], zr.at[q, k],
                     {"col": z + 1 if up else z - 1})

    def n_own(k, to_x):
        src = X.at[0, r, rows_of(k, f)]
        return rcopy(src, src, (nx if to_x else ny).at[k], nr.at[0 if to_x else 1, k], {"row": xn if to_x else yn})

    def n_relay(k, from_x):
        src = X.at[0, xn if from_x else yn, rows_of(k, f)]
        return rcopy(src, src, nrl.at[k], nr.at[2, k], {"row": yn if from_x else xn})

    def m_copy(q, k):
        return rcopy(zsrc(q, k), X.at[1, r, rows_of(k, f)], ms.at[q, k], mr.at[r, k], {"row": q})

    def d_copy(m, b, k, core):
        src = X.at[m, b, rows_of(k, core)]
        return rcopy(src, src, ds.at[m, b, k], dr.at[m, b, k], {"freq": other})

    def d_start(m, b, k):
        d_copy(m, b, k, f).start()

    def own_first(k):
        return pltpu.make_async_copy(zsrc(r, k), X.at[1, r, rows_of(k, f)], tl.at[k])

    for i in range(3):
        w_copy(i).start()

    def start_own(k):
        @pl.when(z < cols_n - 1)
        def _():
            z_own(k, True).start()

        @pl.when(z > 0)
        def _():
            z_own(k, False).start()

        n_own(k, True).start()
        n_own(k, False).start()

    def z_arrive(q, k, go_up):
        z_fwd(q, k, go_up).wait_recv()
        if go_up:
            @pl.when(z < cols_n - 1)
            def _():
                z_fwd(q, k, True).start()
        else:
            @pl.when(z > 0)
            def _():
                z_fwd(q, k, False).start()

        @pl.when(q == r)
        def _():
            own_first(k).start()
            own_first(k).wait()
            d_start(1, r, k)

        @pl.when(q != r)
        def _():
            m_copy(q, k).start()

    def multiply(k):
        for b in range(rows_n):
            rows = pl.ds(pl.multiple_of(k * CH, CH), CH)
            first = X[mi, b, rows, :].astype(jnp.float32).T
            weighted = (first * W[b, pl.ds(k, 1), :]).astype(jnp.bfloat16)
            tile = width // 3
            for t in range(3):
                part = pl.ds(t * tile, tile)
                acc[:, part] += jnp.dot(weighted, X[0, b, rows, part], preferred_element_type=jnp.float32)

    start_own(0)
    for i in range(3):
        w_copy(i).wait_recv()

    SKEW = cols_n

    @pl.loop(0, K + SKEW)
    def _(k):
        @pl.when(k + 1 < K)
        def _():
            start_own(k + 1)

        for d in range(1, cols_n):
            kk = k - (d - 1)
            valid = (kk >= 0) & (kk < K)

            @pl.when(valid & (z - d >= 0))
            def _():
                z_arrive(z - d, kk, True)

            @pl.when(valid & (z + d < cols_n))
            def _():
                z_arrive(z + d, kk, False)

        @pl.when(k < K)
        def _():
            n_own(k, True).wait_recv()
            even = lax.rem(k, 2) == 0

            @pl.when(even)
            def _():
                n_relay(k, True).start()

            d_start(0, xn, k)
            n_own(k, False).wait_recv()

            @pl.when(jnp.logical_not(even))
            def _():
                n_relay(k, False).start()

            d_start(0, yn, k)

        @pl.when((k >= 1) & (k - 1 < K))
        def _():
            n_relay(k - 1, True).wait_recv()
            d_start(0, dg, k - 1)

        kl = k - SKEW + 1

        @pl.when((kl >= 0) & (kl < K) & (r != z))
        def _():
            for p in plane:
                rcopy(zsrc(r, kl), X.at[1, p, rows_of(kl, f)], ms.at[r, kl], mr.at[p, kl], {"row": p}).wait_recv()
                d_start(1, p, kl)

        km = k - SKEW

        @pl.when(km >= 0)
        def _():
            for p in plane:
                d_copy(0, p, km, other).wait_recv()

            @pl.when(r != z)
            def _():
                for b in range(rows_n):
                    d_copy(1, b, km, other).wait_recv()

            multiply(km)

    out = pltpu.make_async_copy(acc, o_ref, osem)
    out.start()

    for i in range(3):
        w_copy(i).wait_send()

    @pl.loop(0, K)
    def _(k):
        n_own(k, True).wait_send()
        n_own(k, False).wait_send()
        n_relay(k, True).wait_send()
        for p in plane:
            d_copy(0, p, k, f).wait_send()

        @pl.when(r != z)
        def _():
            for b in range(rows_n):
                d_copy(1, b, k, f).wait_send()

        for q in range(cols_n):
            @pl.when((q <= z) & (z < cols_n - 1))
            def _():
                z_fwd(q, k, True).wait_send()

            @pl.when((q >= z) & (z > 0))
            def _():
                z_fwd(q, k, False).wait_send()

            @pl.when((q != z) & (q != r))
            def _():
                m_copy(q, k).wait_send()

    out.wait()


def gathered_tile(cols_n, coupling, freq_weight):
    depth, width = coupling.shape
    CH = depth // 6
    K = depth // CH
    rows_n = SIDE * SIDE
    dma = pltpu.SemaphoreType.DMA
    return pl.pallas_call(
        functools.partial(kernel, cols_n, K, CH),
        out_shape=jax.ShapeDtypeStruct((width, width), jnp.float32),
        in_specs=[pl.BlockSpec(memory_space=pl.ANY)] * 2,
        out_specs=pl.BlockSpec(memory_space=pl.ANY),
        scratch_shapes=[
            pltpu.VMEM((2, rows_n, depth, width), jnp.bfloat16),
            pltpu.VMEM((cols_n, depth // 2, width), jnp.bfloat16),
            pltpu.VMEM((rows_n, K, CH), jnp.float32),
            pltpu.VMEM((width, width), jnp.float32),
            dma((2,)), dma((3,)), dma((3,)),
            dma((cols_n, K)), dma((cols_n, K)), dma((cols_n, K)), dma((K,)),
            dma((3, K)), dma((K,)), dma((K,)), dma((K,)),
            dma((cols_n, K)), dma((rows_n, K)), dma((2, rows_n, K)), dma((2, rows_n, K)), dma,
        ],
        compiler_params=pltpu.CompilerParams(
            collective_id=0, has_side_effects=True, vmem_limit_bytes=67043328
        ),
    )(coupling, freq_weight.reshape(K, CH))


def on_device(coupling, freq_weight):
    weighted = (coupling.astype(jnp.float32) * freq_weight[:, None]).astype(jnp.bfloat16)
    full_rows = lax.all_gather(weighted, "col", axis=1, tiled=True)
    return lax.psum_scatter(
        lax.dot_general(
            full_rows, coupling, (((0,), (0,)), ((), ())), preferred_element_type=jnp.float32
        ),
        "row",
        scatter_dimension=0,
        tiled=True,
    )


def solution(mesh):
    placed = (P("row", "col"), P(("freq", "row")))
    square = mesh.shape["freq"] == 2 and mesh.shape["row"] == SIDE * SIDE and mesh.shape["col"] == mesh.shape["row"]

    def step(coupling, freq_weight):
        depth, width = coupling.shape
        if square and depth == width and depth % (6 * 256) == 0:
            return gathered_tile(mesh.shape["col"], coupling, freq_weight)
        return on_device(coupling, freq_weight)

    return jax.shard_map(
        step, mesh=mesh, in_specs=placed, out_specs=P(("freq", "row"), "col"), check_vma=False
    )
```

time: 703 us -> 231 us (0.33)
  waiting for transfers between devices: 644 us -> 0 us
  Pallas kernels: 0 us -> 221 us
  matrix products: 36.7 us -> 0 us
  between operations: 13.4 us -> 0.01 us
  local copies, waits for them, and re-layouts: 0 us -> 9.57 us
    all_gather x1 -> x0, waiting for transfers between devices: 324 us -> none  [on_device(): full_rows = lax.all_gather(weighted, 'col', axis=1, tiled=True)]
    reduce_scatter x1 -> x0, waiting for transfers between devices: 321 us -> none  [on_device(): lax.psum_scatter(lax.dot_general(full_rows, coupling, (((0,), (0,)), ((),...]
    pallas_call x0 -> x1, Pallas kernels: none -> 221 us  [gathered_tile(): pl.pallas_call(functools.partial(kernel, cols_n, K, CH), out_shape=jax.Sh...]
    dot_general x1 -> x0, matrix products: 36.7 us -> none  [on_device(): lax.dot_general(full_rows, coupling, (((0,), (0,)), ((), ())), preferred_...]
    unnamed x0 -> x1, local copies, waits for them, and re-layouts: none -> 8.27 us
  transfers between devices with their start and end apart: 2 -> 0, of which waited for: 2 -> 0; matrix products, arithmetic and copies ran while one was open for 0% -> 0% of each run, Pallas kernels for 0% -> 0%
where the time goes in v1:
time: 231 us
  Pallas kernels  221 us (96%)
  local copies, waits for them, and re-layouts  9.57 us (4%)
    pallas_call x1, Pallas kernels, gathered_tile(): pl.pallas_call(functools.partial(kernel, cols_n, K, CH), out_shape=jax.Sh...  221 us
    unnamed x1, local copies, waits for them, and re-layouts  8.27 us

profile of v1, /device:TPU:6, one launch (start us, length us, event | category | flops | bytes accessed | tf_op | source)
XLA Modules:
  0.0 230.7 jit_solution(6856686872448276542)
XLA Ops:
  0.0 1.3 reshape.3.w_ref
  1.3 221.1 %shard_map.28 = f32[1536,1536]{1,0:T(8,128)} custom-call(bf16[1536,1536]{1,0:T(8,128)(2,1)} %c_ref.1, f32[6,256]{1,0:T(8,128)} %reshape.3.w_ref), custom_call_target="tpu_custom_call" | custom-call | tf_op jit(solution)/shard_map/pallas_call | solution.py:252
  222.4 8.3 %copy.4 = f32[1536,1536]{1,0:T(8,128)} copy(f32[1536,1536]{1,0:T(8,128)} %shard_map.28) | data formatting | bytes 18874368

commit v2 on v1

--- a/solution.py
+++ b/solution.py
@@ -12,7 +12,7 @@
 
 
 def kernel(cols_n, K, CH, c_ref, w_ref, o_ref, X, T, W, acc, load, wsend, wrecv, zr, zup, zdn, tl, nr, nx, ny, nrl,
-           ms, mr, ds, dr, osem):
+           ms, mr, ds, dr, bup, bdn, br, osem):
     f = lax.axis_index("freq")
     r = lax.axis_index("row")
     z = lax.axis_index("col")
@@ -52,7 +52,6 @@
     own.start()
     wown = pltpu.make_async_copy(w_ref, W.at[r], load.at[1])
     wown.start()
-    acc[...] = jnp.zeros_like(acc)
     own.wait()
     wown.wait()
     pl.semaphore_wait(barrier, 1 + len(plane) + jnp.where(z > 0, 1, 0) + jnp.where(z < cols_n - 1, 1, 0))
@@ -96,12 +95,33 @@
     for i in range(3):
         w_copy(i).start()
 
+    def b_copy(b, up):
+        return rcopy(X.at[mi, b, rows_of(0, f)], X.at[1, b, rows_of(0, f)], (bup if up else bdn).at[b], br.at[b],
+                     {"col": z + 1 if up else z - 1})
+
+    go_up, go_down = (z >= r) & (z < cols_n - 1), (z <= r) & (z > 0)
+    dist = jnp.where(z > r, z - r, r - z)
+
+    def b_send(b):
+        @pl.when(go_up)
+        def _():
+            b_copy(b, True).start()
+
+        @pl.when(go_down)
+        def _():
+            b_copy(b, False).start()
+
+    def b_arrive(b):
+        b_copy(b, True).wait_recv()
+        b_send(b)
+        d_start(1, b, 0)
+
     def start_own(k):
-        @pl.when(z < cols_n - 1)
+        @pl.when((z < cols_n - 1) & (k > 0))
         def _():
             z_own(k, True).start()
 
-        @pl.when(z > 0)
+        @pl.when((z > 0) & (k > 0))
         def _():
             z_own(k, False).start()
 
@@ -130,16 +150,31 @@
             m_copy(q, k).start()
 
     def multiply(k):
-        for b in range(rows_n):
-            rows = pl.ds(pl.multiple_of(k * CH, CH), CH)
-            first = X[mi, b, rows, :].astype(jnp.float32).T
-            weighted = (first * W[b, pl.ds(k, 1), :]).astype(jnp.bfloat16)
-            tile = width // 3
-            for t in range(3):
-                part = pl.ds(t * tile, tile)
-                acc[:, part] += jnp.dot(weighted, X[0, b, rows, part], preferred_element_type=jnp.float32)
+        rows = pl.ds(pl.multiple_of(k * CH, CH), CH)
+        for t in range(3):
+            part = pl.ds(t * tile, tile)
+            for b in range(rows_n):
+                first = X[mi, b, rows, part].astype(jnp.float32).T
+                weighted = (first * W[b, pl.ds(k, 1), :]).astype(jnp.bfloat16)
+                acc[part, :] += jnp.dot(weighted, X[0, b, rows, :], preferred_element_type=jnp.float32)
+
+            @pl.when(k == K - 1)
+            def _():
+                out_copy(t).start()
+
+    tile = width // 3
+
+    def out_copy(t):
+        part = pl.ds(t * tile, tile)
+        return pltpu.make_async_copy(acc.at[part], o_ref.at[part], osem.at[t])
 
     start_own(0)
+
+    @pl.when(r == z)
+    def _():
+        b_send(r)
+
+    acc[...] = jnp.zeros_like(acc)
     for i in range(3):
         w_copy(i).wait_recv()
 
@@ -153,7 +188,7 @@
 
         for d in range(1, cols_n):
             kk = k - (d - 1)
-            valid = (kk >= 0) & (kk < K)
+            valid = (kk >= 1) & (kk < K)
 
             @pl.when(valid & (z - d >= 0))
             def _():
@@ -173,6 +208,11 @@
                 n_relay(k, True).start()
 
             d_start(0, xn, k)
+
+            @pl.when((k == 0) & (r == z))
+            def _():
+                b_send(xn)
+
             n_own(k, False).wait_recv()
 
             @pl.when(jnp.logical_not(even))
@@ -180,15 +220,33 @@
                 n_relay(k, False).start()
 
             d_start(0, yn, k)
+
+            @pl.when((k == 0) & (r == z))
+            def _():
+                b_send(yn)
+
 
         @pl.when((k >= 1) & (k - 1 < K))
         def _():
             n_relay(k - 1, True).wait_recv()
             d_start(0, dg, k - 1)
 
+            @pl.when((k == 1) & (r == z))
+            def _():
+                b_send(dg)
+
+        @pl.when((r != z) & (k == dist))
+        def _():
+            for b in (r, xn, yn):
+                b_arrive(b)
+
+        @pl.when((r != z) & (k == dist + 1))
+        def _():
+            b_arrive(dg)
+
         kl = k - SKEW + 1
 
-        @pl.when((kl >= 0) & (kl < K) & (r != z))
+        @pl.when((kl >= 1) & (kl < K) & (r != z))
         def _():
             for p in plane:
                 rcopy(zsrc(r, kl), X.at[1, p, rows_of(kl, f)], ms.at[r, kl], mr.at[p, kl], {"row": p}).wait_recv()
@@ -208,11 +266,16 @@
 
             multiply(km)
 
-    out = pltpu.make_async_copy(acc, o_ref, osem)
-    out.start()
-
     for i in range(3):
         w_copy(i).wait_send()
+    for b in range(rows_n):
+        @pl.when(go_up)
+        def _():
+            b_copy(b, True).wait_send()
+
+        @pl.when(go_down)
+        def _():
+            b_copy(b, False).wait_send()
 
     @pl.loop(0, K)
     def _(k):
@@ -228,19 +291,20 @@
                 d_copy(1, b, k, f).wait_send()
 
         for q in range(cols_n):
-            @pl.when((q <= z) & (z < cols_n - 1))
+            @pl.when((k > 0) & (q <= z) & (z < cols_n - 1))
             def _():
                 z_fwd(q, k, True).wait_send()
 
-            @pl.when((q >= z) & (z > 0))
+            @pl.when((k > 0) & (q >= z) & (z > 0))
             def _():
                 z_fwd(q, k, False).wait_send()
 
-            @pl.when((q != z) & (q != r))
+            @pl.when((k > 0) & (q != z) & (q != r))
             def _():
                 m_copy(q, k).wait_send()
 
-    out.wait()
+    for t in range(3):
+        out_copy(t).wait()
 
 
 def gathered_tile(cols_n, coupling, freq_weight):
@@ -262,7 +326,8 @@
             dma((2,)), dma((3,)), dma((3,)),
             dma((cols_n, K)), dma((cols_n, K)), dma((cols_n, K)), dma((K,)),
             dma((3, K)), dma((K,)), dma((K,)), dma((K,)),
-            dma((cols_n, K)), dma((rows_n, K)), dma((2, rows_n, K)), dma((2, rows_n, K)), dma,
+            dma((cols_n, K)), dma((rows_n, K)), dma((2, rows_n, K)), dma((2, rows_n, K)),
+            dma((rows_n,)), dma((rows_n,)), dma((rows_n,)), dma((3,)),
         ],
         compiler_params=pltpu.CompilerParams(
             collective_id=0, has_side_effects=True, vmem_limit_bytes=67043328

time: 231 us -> 215 us (0.931)
  Pallas kernels: 221 us -> 204 us
    pallas_call x1, Pallas kernels: 221 us -> 204 us  [gathered_tile(): pl.pallas_call(functools.partial(kernel, cols_n, K, CH), out_shape=jax.Sh...]
where the time goes in v2:
time: 215 us; the launch traced here: 213 us
  Pallas kernels  204 us (95%)
  local copies, waits for them, and re-layouts  9.57 us (4%)
    pallas_call x1, Pallas kernels, gathered_tile(): pl.pallas_call(functools.partial(kernel, cols_n, K, CH), out_shape=jax.Sh...  204 us
    unnamed x1, local copies, waits for them, and re-layouts  8.27 us

profile of v2, /device:TPU:6, one launch (start us, length us, event | category | flops | bytes accessed | tf_op | source)
XLA Modules:
  0.0 213.3 jit_solution(15528956934535297430)
XLA Ops:
  0.0 1.3 reshape.3.w_ref
  1.3 203.7 %shard_map.28 = f32[1536,1536]{1,0:T(8,128)} custom-call(bf16[1536,1536]{1,0:T(8,128)(2,1)} %c_ref.1, f32[6,256]{1,0:T(8,128)} %reshape.3.w_ref), custom_call_target="tpu_custom_call" | custom-call | tf_op jit(solution)/shard_map/pallas_call | solution.py:316
  205.0 8.3 %copy.4 = f32[1536,1536]{1,0:T(8,128)} copy(f32[1536,1536]{1,0:T(8,128)} %shard_map.28) | data formatting | bytes 18874368
